TPU v7x, 32 devices: a whole 2x2x4 slice. The times are simulated.
32 devices in a mesh: vocab: 8 (over z, y), layer: 4 (over x, core).
Axes of the slice: x: 2, y: 2, z: 4, core: 2. Of those that a mesh axis runs over, the one named last changes fastest.
Arguments:
- residual: bfloat16 [1024, 8192], P('layer', 'vocab'), may hold values from -40 to 40
- gain: bfloat16 [1, 8192], P(None, 'vocab'), may hold values from 0.25 to 1.75
- unembed: bfloat16 [8192, 128256], P(None, ('vocab', 'layer')), may hold values from -0.22097087 to 0.22097087
Outputs:
- log_probs: float32 [1024, 128256], P('layer', 'vocab')
All inputs are finite; a program needn't handle non-finite values.
Results may differ from a plain program's by a relative error of at most 0.0003.
Values may be sent and summed in bfloat16 or wider, within the bound.
A program may use at most 192 MiB of HBM per device.

v0:
```python
import jax
import jax.numpy as jnp
from jax import lax
from jax.sharding import PartitionSpec as P

D = 8192


def joined(shard, axis, combine):
    everything = jax.tree.map(lambda part: lax.all_gather(part, axis), shard)
    initial = jax.tree.map(lambda part: part[0], everything)

    def lap(k, so_far):
        return combine(so_far, jax.tree.map(lambda part: part[k], everything))

    return lax.fori_loop(1, lax.axis_size(axis), lap, initial)


def combine_pairs(earlier, later):
    highest = jnp.maximum(earlier[0], later[0])
    totals = earlier[1] * jnp.exp(earlier[0] - highest) + later[1] * jnp.exp(later[0] - highest)
    return (highest, totals)


def local(residual, gain, unembed):
    full_rows, full_gain = (
        lax.all_gather(residual, "vocab", axis=1, tiled=True),
        lax.all_gather(gain, "vocab", axis=1, tiled=True),
    )
    all_rows = lax.all_gather(full_rows, "layer", axis=0, tiled=True)
    widened = all_rows.astype(jnp.float32)
    squares = jnp.sum(widened * widened, axis=1)
    scaled = (widened * full_gain.astype(jnp.float32)).astype(jnp.bfloat16)
    products = jnp.dot(scaled, unembed, preferred_element_type=jnp.float32)
    inverse = lax.rsqrt(squares / D + 1e-05)
    logits = products * inverse[:, None]
    local_max = jnp.max(logits, axis=1)
    local_sums = jnp.sum(jnp.exp(logits - local_max[:, None]), axis=1)
    highest, totals = joined((local_max, local_sums), ("vocab", "layer"), combine_pairs)
    lse = highest + jnp.log(totals)
    log_values = logits - lse[:, None]
    return lax.all_to_all(log_values, "layer", split_axis=0, concat_axis=1, tiled=True)


def solution(mesh):
    placed = (P("layer", "vocab"), P(None, "vocab"), P(None, ("vocab", "layer")))
    return jax.shard_map(
        local, mesh=mesh, in_specs=placed, out_specs=P("layer", "vocab"), check_vma=False
    )
```

profile of v0, /device:TPU:0, one launch (start us, length us, event | category | flops | bytes accessed | tf_op | source)
XLA Modules:
  0.0 570.1 jit_solution(13721698906693469134)
XLA Ops:
  6.5 0.0 all-gather.5.cloned.1.call-start
  6.5 0.7 all-gather.5.cloned.1.call-update
  7.3 0.0 all-gather.7.cloned.1.call-start
  7.3 77.7 %all-gather.5.cloned.1.call-done = bf16[256,8192]{1,0:T(8,128)(2,1)} async-done(((bf16[256,1024]{1,0:T(8,128)(2,1)}), bf16[256,8192]{1,0:T(8,128)(2,1)}) %all-gather.5.cloned.1.call-update) | async-done | bytes 4194320 | tf_op jit(solution)/shard_map/all_gather | solution.py:27
  85.0 0.0 all-gather.7.cloned.1.call-update
  85.1 30.7 %all_gather.23 = bf16[1,8192]{1,0:T(2,128)(2,1)S(1)} all-gather(bf16[1,1024]{1,0:T(2,128)(2,1)} %param.6), channel_id=1, replica_groups=mesh['vocab'=8,'layer'=4] {'vocab'}, dimensions={1}, use_global_device_ids=true | all-gather | bytes 18432 | tf_op jit(solution)/shard_map/all_gather | solution.py:28
  115.9 75.2 %all-gather.7.cloned.1.call-done = bf16[1024,8192]{1,0:T(8,128)(2,1)} async-done(((bf16[256,8192]{1,0:T(8,128)(2,1)}), bf16[1024,8192]{1,0:T(8,128)(2,1)}) %all-gather.7.cloned.1.call-update) | async-done | bytes 16777232 | tf_op jit(solution)/shard_map/all_gather | solution.py:30
  191.1 7.2 %fusion.1 = f32[1024]{0:T(1024)S(1)} fusion(bf16[1024,8192]{1,0:T(8,128)(2,1)} %all-gather.7.cloned.1.call-done), kind=kLoop, calls=%fused_computation.6 | loop fusion | flops 25164800 | bytes 16781312 | tf_op jit(solution)/shard_map/reduce_sum | solution.py:32
  198.3 79.6 %multiply_reduce_fusion = (f32[1024]{0:T(1024)S(1)}, f32[1024,4008]{0,1:T(8,128)}) fusion(f32[1024]{0:T(1024)S(1)} %add_rsqrt_fusion, bf16[8192,4008]{0,1:T(8,128)(2,1)} %param.7, bf16[1024,8192]{1,0:T(8,128)(2,1)} %all-gather.7.cloned.1.call-done, f32[8192]{0:T(1024)S(1)} %bitcast.21), kind=kOutput, calls=%fused_computation.12 | convolution fusion | flops 67276455936 | bytes 98902016 | tf_op jit(solution)/shard_map/dot_general | solution.py:34
  277.9 8.4 %exponential_reduce_fusion = f32[1024]{0:T(1024)S(1)} fusion(f32[1024,4008]{0,1:T(8,128)} %get-tuple-element.155, f32[1024]{0:T(1024)S(1)} %get-tuple-element.154, f32[1024]{0:T(1024)S(1)} %add_rsqrt_fusion), kind=kLoop, calls=%fused_computation.10 | loop fusion | flops 12311552 | bytes 16429056 | tf_op jit(solution)/shard_map/reduce_sum | solution.py:38
  286.3 40.9 %all-gather.1 = f32[32768]{0:T(1024)S(1)} all-gather(f32[1024]{0:T(1024)S(1)} %exponential_reduce_fusion), channel_id=3, replica_groups=mesh['vocab'=8,'layer'=4] {'vocab','layer'}, dimensions={0}, use_global_device_ids=true | all-gather | bytes 135168 | tf_op jit(solution)/shard_map/all_gather | solution.py:10
  327.2 37.0 %all-gather = f32[32768]{0:T(1024)S(1)} all-gather(f32[1024]{0:T(1024)S(1)} %get-tuple-element.154), channel_id=2, replica_groups=mesh['vocab'=8,'layer'=4] {'vocab','layer'}, dimensions={0}, use_global_device_ids=true | all-gather | bytes 135168 | tf_op jit(solution)/shard_map/all_gather | solution.py:10
  364.2 1.8 while.17
  366.1 7.2 %multiply_subtract_fusion = f32[1024,4008]{0,1:T(8,128)S(1)} fusion(f32[1024,4008]{0,1:T(8,128)} %get-tuple-element.155, f32[1024]{0:T(1024)S(1)} %log_add_fusion, f32[1024]{0:T(1024)S(1)} %add_rsqrt_fusion), kind=kLoop, calls=%fused_computation.11 | loop fusion | flops 8208384 | bytes 32841728 | tf_op jit(solution)/shard_map/sub | solution.py:41
  373.3 1.8 copy.8
  375.1 182.2 %all_to_all.19 = f32[4,256,4008]{1,2,0:T(8,128)S(1)} all-to-all(f32[4,256,4008]{1,2,0:T(8,128)S(1)} %bitcast.17), channel_id=1, replica_groups=mesh['vocab'=8,'layer'=4] {'layer'}, dimensions={0} | all-to-all | bytes 32833536 | tf_op jit(solution)/shard_map/all_to_all | solution.py:42
  557.3 6.0 %copy.19 = f32[256,16032]{0,1:T(8,128)} copy(f32[256,16032]{0,1:T(8,128)S(1)} %bitcast.18) | data formatting | bytes 32833536
  (69 shorter events, 0.9 us)
Async XLA Ops:
  6.5 78.5 %all-gather.5.cloned.1.call-start = ((), (), s32[]{:S(2)}) async-start(), calls=%async_computation.1 | async-start | bytes 4718592 | tf_op jit(solution)/shard_map/all_gather | solution.py:27
  7.3 183.8 %all-gather.7.cloned.1.call-start = ((), (), s32[]{:S(2)}) async-start(), calls=%async_computation.2 | async-start | bytes 20971520 | tf_op jit(solution)/shard_map/all_gather | solution.py:30
Sparse Core Ops, SparseCore 0:
  9.5 75.4 all-gather.4
  86.6 104.4 all-gather.6
where the time goes:
time: 570 us
  blocking collectives  291 us (51%)
  waiting for transfers between devices  154 us (27%)
  matrix products  79.6 us (14%)
  other arithmetic  23.2 us (4%)
  between operations  13.5 us (2%)
  local copies, waits for them, and re-layouts  8.36 us (1%)
    all_to_all x1, blocking collectives, local(): lax.all_to_all(log_values, 'layer', split_axis=0, concat_axis=1, tiled=True)  182 us
    dot_general x1, matrix products, local(): products = jnp.dot(scaled, unembed, preferred_element_type=jnp.float32)  79.6 us
    all_gather x2, blocking collectives, joined(): everything = jax.tree.map(lambda part: lax.all_gather(part, axis), shard)  77.9 us
    all_gather x1, waiting for transfers between devices, local(): lax.all_gather(residual, 'vocab', axis=1, tiled=True)  77.7 us
    all_gather x1, waiting for transfers between devices, local(): all_rows = lax.all_gather(full_rows, 'layer', axis=0, tiled=True)  75.2 us
    all_gather x1, blocking collectives, local(): lax.all_gather(gain, 'vocab', axis=1, tiled=True)  30.7 us
  transfers between devices with their start and end apart: 2, of which 2 were waited for; matrix products, arithmetic and copies ran while one was open for 0% of the time, Pallas kernels for 0%

commit v1 on v0

v1 whole, which is shorter than its diff:
```python
import jax
import jax.numpy as jnp
from jax import lax
from jax.sharding import PartitionSpec as P


def to_partner(value, step, size):
    return lax.ppermute(value, "layer", [(l, l ^ step) for l in range(size)])


def ring_of(size):
    return list(range(0, size, 2)) + list(range(1, size, 2))[::-1]


def ring_gather(block, place):
    size = lax.axis_size("vocab")
    ring = ring_of(size)
    order = jnp.array(ring, jnp.int32)
    where = jnp.array([ring.index(v) for v in range(size)], jnp.int32)[lax.axis_index("vocab")]
    up = [(ring[p], ring[(p + 1) % size]) for p in range(size)]
    down = [(b, a) for a, b in up]
    half, rows = size // 2, block.shape[0]
    place(block, order[where], 0)
    forward = backward = block
    for k in range(1, half + 1):
        if k == half and size % 2 == 0:
            forward, backward = forward[: rows // 2], backward[rows // 2 :]
        forward = lax.ppermute(forward, "vocab", up)
        backward = lax.ppermute(backward, "vocab", down)
        if k == max(half - 1, 1):
            nearly = (forward, backward)
        place(forward, order[(where - k) % size], 0)
        place(backward, order[(where + k) % size], rows - backward.shape[0])
    return nearly


def body(residual, gain, unembed):
    layers = lax.axis_size("layer")
    vocabs = lax.axis_size("vocab")
    rows, depth = residual.shape
    columns = unembed.shape[1]
    me = lax.axis_index("layer")
    width = depth * vocabs

    widened = residual.astype(jnp.float32)
    squares = jnp.sum(widened * widened, axis=1)
    scaled = (widened * gain.astype(jnp.float32)).astype(jnp.bfloat16)

    total = lax.all_gather(squares, "vocab").sum(0)
    own_inverse = lax.rsqrt(total / width + 1e-05)
    inverse = [to_partner(own_inverse, s, layers) if s else own_inverse for s in range(layers)]

    evens = [s for s in range(layers - 2, -1, -2)] if layers > 1 else [0]
    firsts = {s: to_partner(scaled, s, layers) if s else scaled for s in evens}
    full = {}
    after = own_inverse
    for step in evens:
        first, _ = lax.optimization_barrier((firsts[step], after))
        if step == 0:
            full[0] = lax.all_gather(first, "vocab", axis=1, tiled=True)
            break
        steps = [step, step + 1] if layers > 1 else [step]
        for s in steps:
            full[s] = jnp.zeros((rows, width), jnp.bfloat16)

        def place(block, owner, row):
            column = owner * depth
            full[step] = lax.dynamic_update_slice(full[step], block, (row, column))
            if layers > 1:
                other = to_partner(block, 1, layers)
                full[step + 1] = lax.dynamic_update_slice(full[step + 1], other, (row, column))

        after = ring_gather(first, place)

    order = [s for e in evens for s in ([e, e + 1] if layers > 1 else [e])]
    sent, heads = {}, {}
    for at, step in enumerate(order):
        inv = inverse[step]
        if step == 0 and layers > 1:
            full[1] = to_partner(full[0], 1, layers)
        products = lax.dot_general(
            unembed, full[step], (((0,), (1,)), ((), ())), preferred_element_type=jnp.float32
        )
        logits = products * inv[None, :]
        highest = jnp.max(logits, axis=0)
        centre = jnp.mean(logits, axis=0)
        totals = jnp.sum(jnp.exp(logits - highest[None, :]), axis=0)
        head = jnp.stack([highest, totals, centre])
        if step:
            heads[step] = to_partner(head, step, layers)
            short = (logits - centre[None, :]).astype(jnp.float16)
            if at + 1 < len(order) and order[at + 1] in full:
                following = order[at + 1]
                short, full[following] = lax.optimization_barrier((short, full[following]))
            sent[step] = to_partner(short, step, layers)
        else:
            heads[step] = head
            sent[step] = logits

    mine = jnp.stack([heads[s] for s in range(layers)])
    everyone = lax.all_gather(mine, "vocab")
    highest = jnp.max(everyone[:, :, 0], axis=(0, 1))
    totals = jnp.sum(everyone[:, :, 1] * jnp.exp(everyone[:, :, 0] - highest), axis=(0, 1))
    lse = highest + jnp.log(totals)

    out = jnp.zeros((layers, columns, rows), jnp.float32)
    for step in [0] + [s for s in order[::-1] if s]:
        if step:
            value = sent[step].astype(jnp.float32) + (mine[step, 2] - lse)[None, :]
        else:
            value = sent[step] - lse[None, :]
        out = lax.dynamic_update_slice(out, value[None], (me ^ step, 0, 0))
    return out.reshape(layers * columns, rows).T


def solution(mesh):
    placed = (P("layer", "vocab"), P(None, "vocab"), P(None, ("vocab", "layer")))
    return jax.shard_map(
        body, mesh=mesh, in_specs=placed, out_specs=P("layer", "vocab"), check_vma=False
    )
```

time: 570 us -> 275 us (0.48)
  blocking collectives: 291 us -> 51.5 us
  waiting for transfers between devices: 154 us -> 19.7 us
  matrix products: 79.6 us -> 108 us
  local copies, waits for them, and re-layouts: 8.36 us -> 33.9 us
  starting transfers between devices: 0.04 us -> 18.3 us
  between operations: 13.5 us -> 26.5 us
  other arithmetic: 23.2 us -> 16 us
    all_to_all x1 -> x0, blocking collectives: 182 us -> none  [local(): lax.all_to_all(log_values, 'layer', split_axis=0, concat_axis=1, tiled=True)]
    all_gather x2 -> x1, waiting for transfers between devices: 153 us -> 0.01 us  [body(): full[0] = lax.all_gather(first, 'vocab', axis=1, tiled=True)]
    all_gather x3 -> x2, blocking collectives: 109 us -> 51.5 us  [the longest x1 30.7 us: body(): everyone = lax.all_gather(mine, 'vocab')]
    dot_general x1 -> x4, matrix products: 79.6 us -> 108 us  [body(): lax.dot_general(unembed, full[step], (((0,), (1,)), ((), ())), preferred_...]
    ppermute x0 -> x28, waiting for transfers between devices: none -> 19.7 us  [the longest x4 17.5 us: ring_gather(): forward = lax.ppermute(forward, 'vocab', up)]
    dynamic_update_slice x0 -> x18, local copies, waits for them, and re-layouts: none -> 18.9 us  [the longest x9 9.62 us: place(): lax.dynamic_update_slice(full[step + 1], other, (row, column))]
    ppermute x0 -> x28, starting transfers between devices: none -> 18.3 us  [the longest x20 10 us: to_partner(): return lax.ppermute(value, 'layer', [(l, l ^ step) for l in range(size)])]
    reduce_sum x2 -> x6, other arithmetic: 15.6 us -> 4.34 us  [the longest x3 3 us: body(): totals = jnp.sum(jnp.exp(logits - highest[None, :]), axis=0)]
  transfers between devices with their start and end apart: 2 -> 29, of which waited for: 2 -> 5; matrix products, arithmetic and copies ran while one was open for 0% -> 54% of each run, Pallas kernels for 0% -> 0%
where the time goes in v1:
time: 275 us; the launch traced here: 274 us
  matrix products  108 us (39%)
  blocking collectives  51.5 us (19%)
  local copies, waits for them, and re-layouts  33.9 us (12%)
  between operations  26.5 us (10%)
  waiting for transfers between devices  19.7 us (7%)
  starting transfers between devices  18.3 us (7%)
  other arithmetic  16 us (6%)
    dot_general x4, matrix products, body(): lax.dot_general(unembed, full[step], (((0,), (1,)), ((), ())), preferred_...  108 us
    all_gather x1, blocking collectives, body(): everyone = lax.all_gather(mine, 'vocab')  30.7 us
    all_gather x1, blocking collectives, body(): total = lax.all_gather(squares, 'vocab').sum(0)  20.8 us
    ppermute x4, waiting for transfers between devices, ring_gather(): forward = lax.ppermute(forward, 'vocab', up)  17.5 us
    ppermute x20, starting transfers between devices, to_partner(): return lax.ppermute(value, 'layer', [(l, l ^ step) for l in range(size)])  10 us
    dynamic_update_slice x9, local copies, waits for them, and re-layouts, place(): lax.dynamic_update_slice(full[step + 1], other, (row, column))  9.62 us
    dynamic_update_slice x9, local copies, waits for them, and re-layouts, place(): full[step] = lax.dynamic_update_slice(full[step], block, (row, column))  9.31 us
    ppermute x4, starting transfers between devices, ring_gather(): backward = lax.ppermute(backward, 'vocab', down)  7.79 us
  transfers between devices with their start and end apart: 29, of which 5 were waited for; matrix products, arithmetic and copies ran while one was open for 54% of the time, Pallas kernels for 0%

profile of v1, /device:TPU:0, one launch (start us, length us, event | category | flops | bytes accessed | tf_op | source)
XLA Modules:
  0.0 273.6 jit_solution(10540365794164519275)
XLA Ops:
  8.5 3.0 %collective-permute-start = (bf16[256,1024]{1,0:T(8,128)(2,1)S(1)}, bf16[256,1024]{1,0:T(8,128)(2,1)S(1)}, u32[]{:S(2)}, u32[]{:S(2)}) collective-permute-start(bf16[256,1024]{1,0:T(8,128)(2,1)S(1)} %get-tuple-element.13), channel_id=1, source_target_pairs={{0,2},{1,3},{2,0},{3,1},{4,6},{5,7},{6,4},{7,5},{8,10},{9,11},{10,... | collective-permute-start | bytes 1572872 | tf_op jit(solution)/shard_map/ppermute | solution.py:8
  11.5 20.8 %all-gather.2 = f32[8,1,256]{2,1,0:T(1,128)S(1)} all-gather(f32[1,1,256]{2,1,0:T(1,128)S(1)} %bitcast.86), channel_id=2, replica_groups=mesh['vocab'=8,'layer'=4] {'vocab'}, dimensions={0}, use_global_device_ids=true | all-gather | bytes 9216 | tf_op jit(solution)/shard_map/all_gather | solution.py:49
  32.5 2.0 collective-permute-start.2
  34.5 9.8 %collective-permute-done.1 = bf16[256,1024]{1,0:T(8,128)(2,1)} collective-permute-done((bf16[256,1024]{1,0:T(8,128)(2,1)S(1)}, bf16[256,1024]{1,0:T(8,128)(2,1)}, u32[]{:S(2)}, u32[]{:S(2)}) %collective-permute-start.1) | collective-permute-done | bytes 524320 | tf_op jit(solution)/shard_map/ppermute | solution.py:28
  44.4 2.0 collective-permute-start.4
  62.7 2.5 broadcast.83.clone
  66.0 2.4 broadcast.83.clone.1
  69.3 1.9 constant_dynamic-update-slice_fusion.14
  71.2 2.0 collective-permute-start.6
  73.2 1.9 constant_dynamic-update-slice_fusion.13
  75.1 1.9 constant_dynamic-update-slice_fusion.6
  80.1 5.5 %collective-permute-done.5 = bf16[256,1024]{1,0:T(8,128)(2,1)S(1)} collective-permute-done((bf16[256,1024]{1,0:T(8,128)(2,1)S(1)}, bf16[256,1024]{1,0:T(8,128)(2,1)S(1)}, u32[]{:S(2)}, u32[]{:S(2)}) %collective-permute-start.5) | collective-permute-done | bytes 524320 | tf_op jit(solution)/shard_map/ppermute | solution.py:28
  88.7 1.9 constant_dynamic-update-slice_fusion.3
  92.3 2.2 collective-permute-done.7
  96.4 27.3 %fusion.13 = (f32[256]{0:T(256)S(1)}, f32[256,4008]{0,1:T(8,128)S(1)}) fusion(f32[256]{0:T(256)S(1)} %collective-permute-done.9, bf16[256,8192]{1,0:T(8,128)(2,1)} %constant_dynamic-update-slice_fusion.17, bf16[8192,4008]{0,1:T(8,128)(2,1)} %param.7), kind=kOutput, calls=%fused_computation.61 | convolution fusion | flops 16812822528 | bytes 73967616 | tf_op jit(solution)/shard_map/dot_general | solution.py:81
  128.4 26.7 %fusion.14 = (f32[256]{0:T(256)S(1)}, f32[256,4008]{0,1:T(8,128)S(1)}) fusion(f32[256]{0:T(256)S(1)} %collective-permute-done.19, bf16[256,8192]{1,0:T(8,128)(2,1)} %constant_dynamic-update-slice_fusion.16, bf16[8192,4008]{0,1:T(8,128)(2,1)} %param.7), kind=kOutput, calls=%fused_computation.62 | convolution fusion | flops 16812822528 | bytes 73967616 | tf_op jit(solution)/shard_map/dot_general | solution.py:81
  155.9 1.9 fusion.1
  163.6 26.9 %fusion.16 = (f32[256]{0:T(256)S(1)}, f32[256,4008]{0,1:T(8,128)S(1)}) fusion(f32[256]{0:T(256)S(1)} %add_rsqrt_fusion, bf16[256,8192]{1,0:T(8,128)(2,1)} %all-gather.5.cloned.1.call-done, bf16[8192,4008]{0,1:T(8,128)(2,1)} %param.7), kind=kOutput, calls=%fused_computation.64 | convolution fusion | flops 16812822528 | bytes 73967616 | tf_op jit(solution)/shard_map/dot_general | solution.py:81
  190.6 26.7 %fusion.15 = (f32[256]{0:T(256)S(1)}, f32[256,4008]{0,1:T(8,128)S(1)}) fusion(f32[256]{0:T(256)S(1)} %collective-permute-done.21, bf16[256,8192]{1,0:T(8,128)(2,1)} %collective-permute-done.20, bf16[8192,4008]{0,1:T(8,128)(2,1)} %param.7), kind=kOutput, calls=%fused_computation.63 | convolution fusion | flops 16812822528 | bytes 73967616 | tf_op jit(solution)/shard_map/dot_general | solution.py:81
  222.2 30.7 %all-gather.1 = f32[32,3,256]{2,1,0:T(4,128)S(1)} all-gather(f32[4,3,256]{2,1,0:T(4,128)S(1)} %pad_maximum_fusion), channel_id=3, replica_groups=mesh['vocab'=8,'layer'=4] {'vocab'}, dimensions={0}, use_global_device_ids=true | all-gather | bytes 110592 | tf_op jit(solution)/shard_map/all_gather | solution.py:101
  254.5 2.1 bitcast_dynamic-update-slice_fusion.3
  256.6 2.1 bitcast_dynamic-update-slice_fusion.2
  258.7 2.1 bitcast_dynamic-update-slice_fusion.1
  260.8 6.0 %copy-done = f32[4,4008,256]{2,1,0:T(8,128)} copy-done((f32[4,4008,256]{2,1,0:T(8,128)}, f32[4,4008,256]{2,1,0:T(8,128)S(1)}, u32[]{:S(2)}) %copy-start) | copy-done | bytes 16416792
  (100 shorter events, 34.7 us)
Async XLA Ops:
  6.5 151.2 %all-gather.5.cloned.1.call-start = ((), (), s32[]{:S(2)}) async-start(), calls=%async_computation | async-start | bytes 4718592 | tf_op jit(solution)/shard_map/all_gather | solution.py:60
  8.5 23.9 %collective-permute-start = (bf16[256,1024]{1,0:T(8,128)(2,1)S(1)}, bf16[256,1024]{1,0:T(8,128)(2,1)S(1)}, u32[]{:S(2)}, u32[]{:S(2)}) collective-permute-start(bf16[256,1024]{1,0:T(8,128)(2,1)S(1)} %get-tuple-element.13), channel_id=1, source_target_pairs={{0,2},{1,3},{2,0},{3,1},{4,6},{5,7},{6,4},{7,5},{8,10},{9,11},{10,... | collective-permute-start | bytes 1572872 | tf_op jit(solution)/shard_map/ppermute | solution.py:8
  32.4 11.9 %collective-permute-start.1 = (bf16[256,1024]{1,0:T(8,128)(2,1)S(1)}, bf16[256,1024]{1,0:T(8,128)(2,1)}, u32[]{:S(2)}, u32[]{:S(2)}) collective-permute-start(bf16[256,1024]{1,0:T(8,128)(2,1)S(1)} %collective-permute-done), channel_id=1, source_target_pairs={{0,8},{8,16},{16,24},{24,28},{28,20},{20,12},{12,4},{4,0},{1,9},{9... | collective-permute-start | bytes 1572872 | tf_op jit(solution)/shard_map/ppermute | solution.py:28
  32.5 11.9 %collective-permute-start.2 = (bf16[256,1024]{1,0:T(8,128)(2,1)S(1)}, bf16[256,1024]{1,0:T(8,128)(2,1)}, u32[]{:S(2)}, u32[]{:S(2)}) collective-permute-start(bf16[256,1024]{1,0:T(8,128)(2,1)S(1)} %collective-permute-done), channel_id=1, source_target_pairs={{8,0},{16,8},{24,16},{28,24},{20,28},{12,20},{4,12},{0,4},{9,1},{1... | collective-permute-start | bytes 1572872 | tf_op jit(solution)/shard_map/ppermute | solution.py:29
  34.5 31.5 %collective-permute-start.10 = (bf16[256,1024]{1,0:T(8,128)(2,1)S(1)}, bf16[256,1024]{1,0:T(8,128)(2,1)S(1)}, u32[]{:S(2)}, u32[]{:S(2)}) collective-permute-start(bf16[256,1024]{1,0:T(8,128)(2,1)S(1)} %collective-permute-done), channel_id=1, source_target_pairs={{0,1},{1,0},{2,3},{3,2},{4,5},{5,4},{6,7},{7,6},{8,9},{9,8},{10,11... | collective-permute-start | bytes 1572872 | tf_op jit(solution)/shard_map/ppermute | solution.py:8
  44.4 26.8 %collective-permute-start.3 = (bf16[256,1024]{1,0:T(8,128)(2,1)}, bf16[256,1024]{1,0:T(8,128)(2,1)S(1)}, u32[]{:S(2)}, u32[]{:S(2)}) collective-permute-start(bf16[256,1024]{1,0:T(8,128)(2,1)} %collective-permute-done.1), channel_id=1, source_target_pairs={{0,8},{8,16},{16,24},{24,28},{28,20},{20,12},{12,4},{4,0},{1,9},{9... | collective-permute-start | bytes 1572872 | tf_op jit(solution)/shard_map/ppermute | solution.py:28
  44.4 26.9 %collective-permute-start.4 = (bf16[256,1024]{1,0:T(8,128)(2,1)}, bf16[256,1024]{1,0:T(8,128)(2,1)S(1)}, u32[]{:S(2)}, u32[]{:S(2)}) collective-permute-start(bf16[256,1024]{1,0:T(8,128)(2,1)} %collective-permute-done.2), channel_id=1, source_target_pairs={{8,0},{16,8},{24,16},{28,24},{20,28},{12,20},{4,12},{0,4},{9,1},{1... | collective-permute-start | bytes 1572872 | tf_op jit(solution)/shard_map/ppermute | solution.py:29
  46.4 28.7 %collective-permute-start.11 = (bf16[256,1024]{1,0:T(8,128)(2,1)}, bf16[256,1024]{1,0:T(8,128)(2,1)}, u32[]{:S(2)}, u32[]{:S(2)}) collective-permute-start(bf16[256,1024]{1,0:T(8,128)(2,1)} %collective-permute-done.1), channel_id=1, source_target_pairs={{0,1},{1,0},{2,3},{3,2},{4,5},{5,4},{6,7},{7,6},{8,9},{9,8},{10,11... | collective-permute-start | bytes 1572872 | tf_op jit(solution)/shard_map/ppermute | solution.py:8
  62.1 14.9 %collective-permute-start.12 = (bf16[256,1024]{1,0:T(8,128)(2,1)}, bf16[256,1024]{1,0:T(8,128)(2,1)S(1)}, u32[]{:S(2)}, u32[]{:S(2)}) collective-permute-start(bf16[256,1024]{1,0:T(8,128)(2,1)} %collective-permute-done.2), channel_id=1, source_target_pairs={{0,1},{1,0},{2,3},{3,2},{4,5},{5,4},{6,7},{7,6},{8,9},{9,8},{10,11... | collective-permute-start | bytes 1572872 | tf_op jit(solution)/shard_map/ppermute | solution.py:8
  71.2 14.8 %collective-permute-start.13 = (bf16[256,1024]{1,0:T(8,128)(2,1)S(1)}, bf16[256,1024]{1,0:T(8,128)(2,1)S(1)}, u32[]{:S(2)}, u32[]{:S(2)}) collective-permute-start(bf16[256,1024]{1,0:T(8,128)(2,1)S(1)} %collective-permute-done.3), channel_id=1, source_target_pairs={{0,1},{1,0},{2,3},{3,2},{4,5},{5,4},{6,7},{7,6},{8,9},{9,8},{10,11... | collective-permute-start | bytes 1572872 | tf_op jit(solution)/shard_map/ppermute | solution.py:8
  71.2 14.3 %collective-permute-start.5 = (bf16[256,1024]{1,0:T(8,128)(2,1)S(1)}, bf16[256,1024]{1,0:T(8,128)(2,1)S(1)}, u32[]{:S(2)}, u32[]{:S(2)}) collective-permute-start(bf16[256,1024]{1,0:T(8,128)(2,1)S(1)} %collective-permute-done.3), channel_id=1, source_target_pairs={{0,8},{8,16},{16,24},{24,28},{28,20},{20,12},{12,4},{4,0},{1,9},{9... | collective-permute-start | bytes 1572872 | tf_op jit(solution)/shard_map/ppermute | solution.py:28
  71.2 14.3 %collective-permute-start.6 = (bf16[256,1024]{1,0:T(8,128)(2,1)S(1)}, bf16[256,1024]{1,0:T(8,128)(2,1)S(1)}, u32[]{:S(2)}, u32[]{:S(2)}) collective-permute-start(bf16[256,1024]{1,0:T(8,128)(2,1)S(1)} %collective-permute-done.4), channel_id=1, source_target_pairs={{8,0},{16,8},{24,16},{28,24},{20,28},{12,20},{4,12},{0,4},{9,1},{1... | collective-permute-start | bytes 1572872 | tf_op jit(solution)/shard_map/ppermute | solution.py:29
  75.1 13.5 %collective-permute-start.14 = (bf16[256,1024]{1,0:T(8,128)(2,1)S(1)}, bf16[256,1024]{1,0:T(8,128)(2,1)}, u32[]{:S(2)}, u32[]{:S(2)}) collective-permute-start(bf16[256,1024]{1,0:T(8,128)(2,1)S(1)} %collective-permute-done.4), channel_id=1, source_target_pairs={{0,1},{1,0},{2,3},{3,2},{4,5},{5,4},{6,7},{7,6},{8,9},{9,8},{10,11... | collective-permute-start | bytes 1572872 | tf_op jit(solution)/shard_map/ppermute | solution.py:8
  77.1 19.4 %collective-permute-start.9 = (f32[256]{0:T(256)S(1)}, f32[256]{0:T(256)S(1)}, u32[]{:S(2)}, u32[]{:S(2)}) collective-permute-start(f32[256]{0:T(256)S(1)} %add_rsqrt_fusion), channel_id=1, source_target_pairs={{0,2},{1,3},{2,0},{3,1},{4,6},{5,7},{6,4},{7,5},{8,10},{9,11},{10,... | collective-permute-start | bytes 3080 | tf_op jit(solution)/shard_map/ppermute | solution.py:8
  85.5 42.8 %collective-permute-start.19 = (f32[256]{0:T(256)S(1)}, f32[256]{0:T(256)S(1)}, u32[]{:S(2)}, u32[]{:S(2)}) collective-permute-start(f32[256]{0:T(256)S(1)} %add_rsqrt_fusion), channel_id=1, source_target_pairs={{0,3},{1,2},{2,1},{3,0},{4,7},{5,6},{6,5},{7,4},{8,11},{9,10},{10,... | collective-permute-start | bytes 3080 | tf_op jit(solution)/shard_map/ppermute | solution.py:8
  86.0 9.2 %collective-permute-start.8 = (bf16[128,1024]{1,0:T(8,128)(2,1)S(1)}, bf16[128,1024]{1,0:T(8,128)(2,1)S(1)}, u32[]{:S(2)}, u32[]{:S(2)}) collective-permute-start(bf16[128,1024]{1,0:T(8,128)(2,1)S(1)} %slice.30), channel_id=1, source_target_pairs={{8,0},{16,8},{24,16},{28,24},{20,28},{12,20},{4,12},{0,4},{9,1},{1... | collective-permute-start | bytes 786440 | tf_op jit(solution)/shard_map/ppermute | solution.py:29
  88.6 36.5 %collective-permute-start.15 = (bf16[256,1024]{1,0:T(8,128)(2,1)S(1)}, bf16[256,1024]{1,0:T(8,128)(2,1)S(1)}, u32[]{:S(2)}, u32[]{:S(2)}) collective-permute-start(bf16[256,1024]{1,0:T(8,128)(2,1)S(1)} %collective-permute-done.5), channel_id=1, source_target_pairs={{0,1},{1,0},{2,3},{3,2},{4,5},{5,4},{6,7},{7,6},{8,9},{9,8},{10,11... | collective-permute-start | bytes 1572872 | tf_op jit(solution)/shard_map/ppermute | solution.py:8
  94.5 31.5 %collective-permute-start.16 = (bf16[256,1024]{1,0:T(8,128)(2,1)S(1)}, bf16[256,1024]{1,0:T(8,128)(2,1)S(1)}, u32[]{:S(2)}, u32[]{:S(2)}) collective-permute-start(bf16[256,1024]{1,0:T(8,128)(2,1)S(1)} %collective-permute-done.6), channel_id=1, source_target_pairs={{0,1},{1,0},{2,3},{3,2},{4,5},{5,4},{6,7},{7,6},{8,9},{9,8},{10,11... | collective-permute-start | bytes 1572872 | tf_op jit(solution)/shard_map/ppermute | solution.py:8
  95.2 31.7 %collective-permute-start.17 = (bf16[128,1024]{1,0:T(8,128)(2,1)S(1)}, bf16[128,1024]{1,0:T(8,128)(2,1)S(1)}, u32[]{:S(2)}, u32[]{:S(2)}) collective-permute-start(bf16[128,1024]{1,0:T(8,128)(2,1)S(1)} %collective-permute-done.7), channel_id=1, source_target_pairs={{0,1},{1,0},{2,3},{3,2},{4,5},{5,4},{6,7},{7,6},{8,9},{9,8},{10,11... | collective-permute-start | bytes 786440 | tf_op jit(solution)/shard_map/ppermute | solution.py:8
  157.8 32.9 %collective-permute-start.20 = (bf16[256,8192]{1,0:T(8,128)(2,1)}, bf16[256,8192]{1,0:T(8,128)(2,1)}, u32[]{:S(2)}, u32[]{:S(2)}) collective-permute-start(bf16[256,8192]{1,0:T(8,128)(2,1)} %all-gather.5.cloned.1.call-done), channel_id=1, source_target_pairs={{0,1},{1,0},{2,3},{3,2},{4,5},{5,4},{6,7},{7,6},{8,9},{9,8},{10,11... | collective-permute-start | bytes 12582920 | tf_op jit(solution)/shard_map/ppermute | solution.py:8
  160.0 30.6 %collective-permute-start.21 = (f32[256]{0:T(256)S(1)}, f32[256]{0:T(256)S(1)}, u32[]{:S(2)}, u32[]{:S(2)}) collective-permute-start(f32[256]{0:T(256)S(1)} %add_rsqrt_fusion), channel_id=1, source_target_pairs={{0,1},{1,0},{2,3},{3,2},{4,5},{5,4},{6,7},{7,6},{8,9},{9,8},{10,11... | collective-permute-start | bytes 3080 | tf_op jit(solution)/shard_map/ppermute | solution.py:8
  162.1 96.6 %collective-permute-start.27 = (f16[4008,256]{1,0:T(8,128)(2,1)S(1)}, f16[4008,256]{1,0:T(8,128)(2,1)}, u32[]{:S(2)}, u32[]{:S(2)}) collective-permute-start(f16[4008,256]{1,0:T(8,128)(2,1)S(1)} %fusion), channel_id=1, source_target_pairs={{0,2},{1,3},{2,0},{3,1},{4,6},{5,7},{6,4},{7,5},{8,10},{9,11},{10,... | collective-permute-start | bytes 6156296 | tf_op jit(solution)/shard_map/ppermute | solution.py:8
  190.5 66.1 %collective-permute-start.26 = (f16[4008,256]{1,0:T(8,128)(2,1)}, f16[4008,256]{1,0:T(8,128)(2,1)}, u32[]{:S(2)}, u32[]{:S(2)}) collective-permute-start(f16[4008,256]{1,0:T(8,128)(2,1)} %fusion.1), channel_id=1, source_target_pairs={{0,3},{1,2},{2,1},{3,0},{4,7},{5,6},{6,5},{7,4},{8,11},{9,10},{10,... | collective-permute-start | bytes 6156296 | tf_op jit(solution)/shard_map/ppermute | solution.py:8
  221.4 33.2 %collective-permute-start.25 = (f16[4008,256]{1,0:T(8,128)(2,1)}, f16[4008,256]{1,0:T(8,128)(2,1)}, u32[]{:S(2)}, u32[]{:S(2)}) collective-permute-start(f16[4008,256]{1,0:T(8,128)(2,1)} %fusion.2), channel_id=1, source_target_pairs={{0,1},{1,0},{2,3},{3,2},{4,5},{5,4},{6,7},{7,6},{8,9},{9,8},{10,11... | collective-permute-start | bytes 6156296 | tf_op jit(solution)/shard_map/ppermute | solution.py:8
  (7 other events, 86.3 us)
Sparse Core Ops, SparseCore 0:
  86.1 71.3 all-gather.4
